TPU v7x, 128 devices: a whole 4x4x4 slice. The times are simulated.
128 devices in a mesh: owner: 8 (over x, core), server: 16 (over z, y).
Axes of the slice: x: 4, y: 4, z: 4, core: 2. Of those that a mesh axis runs over, the one named last changes fastest.
Arguments:
- queries: bfloat16 [32768, 1024], P(('owner', 'server')), may hold values from -8 to 8
- key_vectors: bfloat16 [32768, 128], P(('owner', 'server')), may hold values from -8 to 8
- value_vectors: bfloat16 [32768, 128], P(('owner', 'server')), may hold values from -6 to 6
- out_grad: bfloat16 [32768, 1024], P(('owner', 'server')), may hold values from -6 to 6
- segments: int32 [32768], replicated, may hold values from 0 to 31, never falling along the last dimension, each value on 1 to 2048 neighbouring positions
- phase_label: int32 [128], P(('owner', 'server')), may hold values 0 or 1
Outputs:
- attn_out: bfloat16 [32768, 1024], P(('owner', 'server'))
- grad_query: bfloat16 [32768, 1024], P(('owner', 'server'))
- grad_key: float32 [32768, 128], P(('owner', 'server'))
- grad_value: float32 [32768, 128], P(('owner', 'server'))
All inputs are finite; a program needn't handle non-finite values. No bound on the sum of `phase_label` on one device may be relied on, other than what follows from the above.
Results may differ from a plain program's by a relative error of at most 0.012.
The roundings to bfloat16 on the way count: a program that leaves them out, or rounds other values in their place, can miss the bound.
Values may be sent and summed in bfloat16 or wider, within the bound.
A program may use at most 128 MiB of HBM per device.

v0:
```python
import functools
import math

import jax
import jax.numpy as jnp
from jax import lax
from jax.experimental import pallas as pl
from jax.experimental.pallas import tpu as pltpu
from jax.sharding import PartitionSpec as P

MESH = pl.DeviceIdType.MESH
REACH = 8
SLOTS = REACH + 1
ROW = 4
FAR = -1e30
UNROLL_F = 2
UNROLL_B = 2
F32 = jnp.float32
BF16 = jnp.bfloat16


def fused(
    heads, scale, servers, tiles,
    q_hbm, k_hbm, v_hbm, do_hbm, seg_ref, phase_ref,
    o_ref, dq_ref, dk_ref, dv_ref,
    q_s, do_s, qt_s, dot_s, win, win_t, s_s, dp_s, bias_s, m_s, l_s, d_s, ot_s, dqt_s,
    acc, out_buf, in_buf,
    load_sem, fsend, frecv, bsend, brecv,
):
    tok, width = q_s.shape[1], q_s.shape[2]
    owner = lax.axis_index("owner")
    server = lax.axis_index("server")
    tile = owner * servers + server
    y = server % ROW
    first, last = (y + 3) // 4, y // 3

    def at_tile(t):
        t = (t + tiles) % tiles
        return (t // servers, t % servers)

    up, down = at_tile(tile + ROW), at_tile(tile - ROW)
    row_start = server - y
    right = (owner, row_start + (y + 1) % ROW)
    left = (owner, row_start + (y + 3) % ROW)

    loads = [pltpu.make_async_copy(k_hbm, win.at[0, 0], load_sem.at[0]),
             pltpu.make_async_copy(v_hbm, win.at[0, 1], load_sem.at[1])]
    for h in range(heads):
        cols = pl.ds(h * width, width)
        loads.append(pltpu.make_async_copy(q_hbm.at[:, cols], q_s.at[h], load_sem.at[2 + h]))
        loads.append(pltpu.make_async_copy(do_hbm.at[:, cols], do_s.at[h], load_sem.at[2 + heads + h]))
    for copy in loads:
        copy.start()

    barrier = pltpu.get_barrier_semaphore()
    for peer in (up, down, left, right):
        pl.semaphore_signal(barrier, inc=1, device_id=peer, device_id_type=MESH)
    pl.semaphore_wait(barrier, 4)

    def block(src, dst, send, half, peer):
        return pltpu.make_async_remote_copy(
            src_ref=win.at[src, half], dst_ref=win.at[dst, half],
            send_sem=fsend.at[send, half], recv_sem=frecv.at[dst, half],
            device_id=peer, device_id_type=MESH)

    def send_block(src, dst, send, peer):
        for half in range(2):
            block(src, dst, send, half, peer).start()

    def wait_block(slot):
        for half in range(2):
            block(slot, slot, 0, half, left).wait_recv()

    loads[0].wait()
    loads[1].wait()
    send_block(0, 4, 0, up)

    @pl.when(y != 3)
    def _():
        send_block(0, 1, 1, right)

    @pl.when(y == 0)
    def _():
        send_block(0, 3, 2, left)

    for copy in loads[2:]:
        copy.wait()
    for h in range(heads):
        qt_s[h] = q_s[h].T
        dot_s[h] = do_s[h].T

    log2e = 1.4426950408889634
    q_seg = seg_ref[pl.ds(tile, 1), :]

    def forward(slot):
        owner_tile = tile - slot
        k_seg = seg_ref[pl.ds((owner_tile + tiles) % tiles, 1), :]
        k_seg = jnp.where(owner_tile >= 0, k_seg, -1)
        k_col = jnp.broadcast_to(k_seg.astype(F32), (128, tok)).T
        k_col = jnp.concatenate([k_col] * (tok // 128), axis=1)
        seen = k_col == q_seg.astype(F32)
        if slot == 0:
            key_at = lax.broadcasted_iota(jnp.int32, (tok, tok), 0)
            query_at = lax.broadcasted_iota(jnp.int32, (tok, tok), 1)
            seen = seen & (key_at <= query_at)
        bias_s[...] = jnp.where(seen, 0.0, FAR)
        win_t[slot, 0] = win[slot, 0].T
        win_t[slot, 1] = win[slot, 1].T

        def some_heads(step, carry):
            for part in range(UNROLL_F):
                h = step * UNROLL_F + part
                s = jnp.dot(win[slot, 0], qt_s[h], preferred_element_type=F32)
                s = s * (scale * log2e) + bias_s[...]
                s_s[slot, h] = s
                top = jnp.max(s, axis=0, keepdims=True)
                if slot == 0:
                    p = jnp.exp2(s - top)
                    l_s[h] = jnp.sum(p, axis=0, keepdims=True)
                    ot_s[h] = jnp.dot(win_t[slot, 1], p.astype(BF16), preferred_element_type=F32)
                    m_s[h] = top
                else:
                    old = m_s[h]
                    top = jnp.maximum(old, top)
                    shrink = jnp.exp2(old - top)
                    p = jnp.exp2(s - top)
                    l_s[h] = l_s[h] * shrink + jnp.sum(p, axis=0, keepdims=True)
                    ot_s[h] = ot_s[h] * shrink + jnp.dot(
                        win_t[slot, 1], p.astype(BF16), preferred_element_type=F32)
                    m_s[h] = top
                dp_s[slot, h] = jnp.dot(win[slot, 1], dot_s[h], preferred_element_type=F32)
            return carry

        lax.fori_loop(0, heads // UNROLL_F, some_heads, 0)

    forward(0)

    wait_block(4)
    send_block(4, 8, 3, up)

    @pl.when(y == 3)
    def _():
        send_block(4, 1, 1, right)

    @pl.when(y != 0)
    def _():
        send_block(4, 3, 2, left)

    @pl.when(y != 3)
    def _():
        send_block(4, 5, 4, right)

    @pl.when(y == 0)
    def _():
        send_block(4, 7, 5, left)

    forward(4)

    wait_block(1)

    @pl.when(y != 3)
    def _():
        send_block(1, 2, 6, right)

    forward(1)

    wait_block(8)

    @pl.when(y == 3)
    def _():
        send_block(8, 5, 4, right)

    @pl.when(y != 0)
    def _():
        send_block(8, 7, 5, left)

    wait_block(3)

    @pl.when(y == 0)
    def _():
        send_block(3, 6, 7, left)

    forward(3)
    wait_block(5)

    @pl.when(y == 3)
    def _():
        send_block(5, 2, 6, right)

    forward(8)
    wait_block(7)

    @pl.when(y != 0)
    def _():
        send_block(7, 6, 7, left)

    forward(5)
    forward(7)
    wait_block(2)
    forward(2)
    wait_block(6)
    forward(6)

    def finish_head(h, carry):
        total = l_s[h]
        out_t = (ot_s[h] / total).astype(BF16)
        d_s[h] = jnp.sum(dot_s[h].astype(F32) * out_t.astype(F32), axis=0, keepdims=True)
        m_s[h] = m_s[h] + jnp.log2(total)
        cols = pl.ds(pl.multiple_of(h * width, width), width)
        o_ref[:, cols] = out_t.T
        return carry

    lax.fori_loop(0, heads, finish_head, 0)

    def backward(slot, first_slot=False):
        def some_heads(step, carry):
            key_part = None
            for part in range(UNROLL_B):
                h = step * UNROLL_B + part
                p = jnp.exp2(s_s[slot, h] - m_s[h])
                ds = (p * (dp_s[slot, h] - d_s[h])).astype(BF16)
                pb = p.astype(BF16)
                dq = jnp.dot(win_t[slot, 0], ds, preferred_element_type=F32)
                if first_slot:
                    dqt_s[h] = dq
                else:
                    dqt_s[h] = dqt_s[h] + dq
                dk = jnp.dot(ds, q_s[h], preferred_element_type=F32)
                dv = jnp.dot(pb, do_s[h], preferred_element_type=F32)
                key_part = dk if key_part is None else key_part + dk
                value_part = dv if part == 0 else value_part + dv
            return (carry[0] + key_part, carry[1] + value_part)

        zero = jnp.zeros((tok, width), F32)
        dk, dv = lax.fori_loop(0, heads // UNROLL_B, some_heads, (zero, zero))
        flag = phase_ref[0].astype(F32)
        acc[slot, 0] = dk * (scale * flag)
        acc[slot, 1] = dv * flag

    def part(slot, half, peer):
        return pltpu.make_async_remote_copy(
            src_ref=out_buf.at[slot, half], dst_ref=in_buf.at[slot, half],
            send_sem=bsend.at[slot, half], recv_sem=brecv.at[slot, half],
            device_id=peer, device_id_type=MESH)

    def send_half(slot, half, peer):
        out_buf[slot, half] = acc[slot, half].astype(BF16)
        part(slot, half, peer).start()

    def send_part(slot, peer):
        for half in range(2):
            send_half(slot, half, peer)

    def take_half(slot, into, half):
        part(slot, half, left).wait_recv()
        acc[into, half] = acc[into, half] + in_buf[slot, half].astype(F32)

    backward(2, True)
    send_part(2, left)
    backward(6)
    send_part(6, right)
    backward(1)
    backward(5)
    send_part(5 - 4 * last, left)
    backward(3)
    backward(7)
    send_part(7 - 4 * first, right)
    for half in range(2):
        take_half(2, 1 + 4 * last, half)
        send_half(1 + 4 * last, half, left)
        take_half(6, 3 + 4 * first, half)
        send_half(3 + 4 * first, half, right)
    backward(8)
    backward(4)
    backward(0)

    def finish_query(h, carry):
        flag = phase_ref[0].astype(F32)
        cols = pl.ds(pl.multiple_of(h * width, width), width)
        dq_ref[:, cols] = (dqt_s[h] * (scale * flag)).astype(BF16).T
        return carry

    lax.fori_loop(0, heads, finish_query, 0)

    for half in range(2):
        take_half(5, 4 + 4 * last, half)
        take_half(7, 4 + 4 * first, half)
        take_half(1, 4 * last, half)
        take_half(3, 4 * first, half)
        send_half(8, half, down)
    for half in range(2):
        take_half(8, 4, half)
        send_half(4, half, down)
    for half in range(2):
        take_half(4, 0, half)
    dk_ref[...] = acc[0, 0]
    dv_ref[...] = acc[0, 1]

    for half in range(2):
        for send in range(8):
            block(0, 0, send, half, left).wait_send()
        for slot in range(1, SLOTS):
            part(slot, half, left).wait_send()


def solution(mesh):
    servers = mesh.shape["server"]
    tiles = servers * mesh.shape["owner"]

    def on_device(queries, key_vectors, value_vectors, out_grad, segments, phase_label):
        tok, width = key_vectors.shape
        heads = queries.shape[1] // width
        seg_rows = segments.reshape(tiles, tok)
        vmem = pl.BlockSpec(memory_space=pltpu.VMEM)
        anywhere = pl.BlockSpec(memory_space=pl.ANY)
        smem = pl.BlockSpec(memory_space=pltpu.SMEM)
        return pl.pallas_call(
            functools.partial(fused, heads, 1.0 / math.sqrt(width), servers, tiles),
            out_shape=(
                jax.ShapeDtypeStruct((tok, heads * width), BF16),
                jax.ShapeDtypeStruct((tok, heads * width), BF16),
                jax.ShapeDtypeStruct((tok, width), F32),
                jax.ShapeDtypeStruct((tok, width), F32),
            ),
            in_specs=[anywhere, anywhere, anywhere, anywhere, vmem, smem],
            out_specs=(vmem, vmem, vmem, vmem),
            scratch_shapes=[
                pltpu.VMEM((heads, tok, width), BF16),
                pltpu.VMEM((heads, tok, width), BF16),
                pltpu.VMEM((heads, width, tok), BF16),
                pltpu.VMEM((heads, width, tok), BF16),
                pltpu.VMEM((SLOTS, 2, tok, width), BF16),
                pltpu.VMEM((SLOTS, 2, width, tok), BF16),
                pltpu.VMEM((SLOTS, heads, tok, tok), F32),
                pltpu.VMEM((SLOTS, heads, tok, tok), F32),
                pltpu.VMEM((tok, tok), F32),
                pltpu.VMEM((heads, 1, tok), F32),
                pltpu.VMEM((heads, 1, tok), F32),
                pltpu.VMEM((heads, 1, tok), F32),
                pltpu.VMEM((heads, width, tok), F32),
                pltpu.VMEM((heads, width, tok), F32),
                pltpu.VMEM((SLOTS, 2, tok, width), F32),
                pltpu.VMEM((SLOTS, 2, tok, width), BF16),
                pltpu.VMEM((SLOTS, 2, tok, width), BF16),
                pltpu.SemaphoreType.DMA((2 + 2 * heads,)),
                pltpu.SemaphoreType.DMA((8, 2)),
                pltpu.SemaphoreType.DMA((SLOTS, 2)),
                pltpu.SemaphoreType.DMA((SLOTS, 2)),
                pltpu.SemaphoreType.DMA((SLOTS, 2)),
            ],
            compiler_params=pltpu.CompilerParams(
                collective_id=0, has_side_effects=True, vmem_limit_bytes=60 * 1024 * 1024
            ),
        )(queries, key_vectors, value_vectors, out_grad, seg_rows, phase_label)

    tokens = P(("owner", "server"), None)
    return jax.shard_map(
        on_device,
        mesh=mesh,
        in_specs=(tokens, tokens, tokens, tokens, P(), P(("owner", "server"))),
        out_specs=(tokens, tokens, tokens, tokens),
        check_vma=False,
    )
```

profile of v0, /device:TPU:97, one launch (start us, length us, event | category | flops | bytes accessed | tf_op | source)
XLA Modules:
  0.0 66.0 jit_solution(11296240155547772625)
XLA Ops:
  1.3 1.6 %reshape.11.seg_ref = s32[128,256]{1,0:T(8,128)} reshape(s32[32768]{0:T(1024)} %param.10) | data formatting | bytes 262144 | tf_op jit(solution)/shard_map/reshape | solution.py:313
  2.9 58.5 %shard_map.93 = (bf16[256,1024]{1,0:T(8,128)(2,1)}, bf16[256,1024]{1,0:T(8,128)(2,1)}, f32[256,128]{1,0:T(8,128)}, f32[256,128]{1,0:T(8,128)}) custom-call(bf16[256,1024]{1,0:T(8,128)(2,1)} %q_hbm.1, bf16[256,128]{1,0:T(8,128)(2,1)} %k_hbm.1, bf16[256,128]{1,0:T(8,128)(2,1)} %v_hbm.1, bf16[256,1024]{1,0:T(8,128)(2,1)} %do_hbm.1, ...), custom_call_target="tpu_custom_call" | custom-call | tf_op jit(solution)/shard_map/pallas_call | solution.py:317
  61.4 0.0 copy-start
  61.4 1.9 %copy.15 = bf16[256,1024]{1,0:T(8,128)(2,1)} copy(bf16[256,1024]{1,0:T(8,128)(2,1)} %get-tuple-element.8) | data formatting | bytes 1048576
  63.4 0.0 copy-done
  63.4 0.0 copy-start.2
  63.4 0.8 %copy.16 = bf16[256,1024]{1,0:T(8,128)(2,1)} copy(bf16[256,1024]{1,0:T(8,128)(2,1)S(1)} %copy-done) | data formatting | bytes 1048576
  64.2 0.2 copy-done.2
  64.4 0.0 copy-start.1
  64.4 0.7 copy.17
  65.0 0.3 copy-done.1
  65.3 0.7 copy.18
Async XLA Ops:
  61.4 1.9 %copy-start = (bf16[256,1024]{1,0:T(8,128)(2,1)S(1)}, bf16[256,1024]{1,0:T(8,128)(2,1)}, u32[]{:S(2)}) copy-start(bf16[256,1024]{1,0:T(8,128)(2,1)} %get-tuple-element.9) | copy-start | bytes 1572868
  63.4 1.0 %copy-start.2 = (f32[256,128]{1,0:T(8,128)S(1)}, f32[256,128]{1,0:T(8,128)}, u32[]{:S(2)}) copy-start(f32[256,128]{1,0:T(8,128)} %get-tuple-element.10) | copy-start | bytes 393220
  64.4 1.0 %copy-start.1 = (f32[256,128]{1,0:T(8,128)S(1)}, f32[256,128]{1,0:T(8,128)}, u32[]{:S(2)}) copy-start(f32[256,128]{1,0:T(8,128)} %get-tuple-element.11) | copy-start | bytes 393220
where the time goes:
time: 66.2 us; the launch traced here: 66 us
  Pallas kernels  58.5 us (88%)
  local copies, waits for them, and re-layouts  6.15 us (9%)
  between operations  1.3 us (2%)
    pallas_call x1, Pallas kernels, on_device(): pl.pallas_call(functools.partial(fused, heads, 1.0 / math.sqrt(width), se...  58.5 us
    unnamed x10, local copies, waits for them, and re-layouts  4.56 us
    reshape x1, local copies, waits for them, and re-layouts, on_device(): seg_rows = segments.reshape(tiles, tok)  1.6 us

commit v1 on v0

v1 whole, which is shorter than its diff:
```python
import functools
import math

import jax
import jax.numpy as jnp
from jax import lax
from jax.experimental import pallas as pl
from jax.experimental.pallas import tpu as pltpu
from jax.sharding import PartitionSpec as P

MESH = pl.DeviceIdType.MESH
REACH = 8
SLOTS = REACH + 1
ROW = 4
FAR = -1e30
LAG = 3
CUTS = 2
F32 = jnp.float32
BF16 = jnp.bfloat16


def fused(
    heads, scale, servers, tiles,
    q_hbm, k_hbm, v_hbm, do_hbm, seg_hbm, phase_ref,
    o_ref, dq_ref, dk_ref, dv_ref,
    q_s, do_s, qt_s, dot_s, win, win_t, seg_s, s_s, dp_s, bias_s, m_s, l_s, d_s, ot_s, outt_s, dqt_s,
    acc, out_buf, in_buf,
    load_sem, fsend, frecv, bsend, brecv,
):
    tok, width = q_s.shape[1], q_s.shape[2]
    owner = lax.axis_index("owner")
    server = lax.axis_index("server")
    tile = owner * servers + server
    y = server % ROW
    first, last = (y + 3) // 4, y // 3
    rows_of = [pl.ds(k * (tok // CUTS), tok // CUTS) for k in range(CUTS)]
    pieces = [(half, cut) for half in range(2) for cut in range(CUTS)]

    def at_tile(t):
        t = (t + tiles) % tiles
        return (t // servers, t % servers)

    up, down = at_tile(tile + ROW), at_tile(tile - ROW)
    row_start = server - y
    right = (owner, row_start + (y + 1) % ROW)
    left = (owner, row_start + (y + 3) % ROW)

    loads = [pltpu.make_async_copy(k_hbm, win.at[0, 0], load_sem.at[0]),
             pltpu.make_async_copy(v_hbm, win.at[0, 1], load_sem.at[1]),
             pltpu.make_async_copy(seg_hbm, seg_s, load_sem.at[2])]
    for h in range(heads):
        cols = pl.ds(h * width, width)
        loads.append(pltpu.make_async_copy(q_hbm.at[:, cols], q_s.at[h], load_sem.at[3 + h]))
        loads.append(pltpu.make_async_copy(do_hbm.at[:, cols], do_s.at[h], load_sem.at[3 + heads + h]))
    for copy in loads:
        copy.start()

    barrier = pltpu.get_barrier_semaphore()
    for peer in (up, down, left, right):
        pl.semaphore_signal(barrier, inc=1, device_id=peer, device_id_type=MESH)
    pl.semaphore_wait(barrier, 4)

    def block(src, dst, send, half, cut, peer):
        return pltpu.make_async_remote_copy(
            src_ref=win.at[src, half, rows_of[cut]], dst_ref=win.at[dst, half, rows_of[cut]],
            send_sem=fsend.at[send, half, cut], recv_sem=frecv.at[dst, half, cut],
            device_id=peer, device_id_type=MESH)

    def pass_on(slot, *moves):
        for half, cut in pieces:
            if slot:
                block(slot, slot, 0, half, cut, left).wait_recv()
            elif cut == 0:
                loads[half].wait()
            for when, dst, send, peer in moves:
                if when is None:
                    block(slot, dst, send, half, cut, peer).start()
                else:
                    @pl.when(when)
                    def _():
                        block(slot, dst, send, half, cut, peer).start()

    pass_on(0, (None, 4, 0, up), (y != 3, 1, 1, right), (y == 0, 3, 2, left))

    for copy in loads[2:]:
        copy.wait()
    for h in range(heads):
        qt_s[h] = q_s[h].T
        dot_s[h] = do_s[h].T

    log2e = 1.4426950408889634
    seg_rows = tok // 128

    def seg_row(t):
        parts = [seg_s[pl.ds(t * seg_rows + k, 1), :] for k in range(seg_rows)]
        return jnp.concatenate(parts, axis=1)

    q_seg = seg_row(tile).astype(F32)

    def eight_rows(x, op):
        total = x[0:8]
        for k in range(1, x.shape[0] // 8):
            total = op(total, x[k * 8:(k + 1) * 8])
        return total

    def forward(slot):
        owner_tile = tile - slot
        k_seg = seg_row((owner_tile + tiles) % tiles)
        k_seg = jnp.where(owner_tile >= 0, k_seg, -1)
        k_col = jnp.broadcast_to(k_seg.astype(F32), (128, tok)).T
        k_col = jnp.concatenate([k_col] * (tok // 128), axis=1)
        seen = k_col == q_seg
        if slot == 0:
            key_at = lax.broadcasted_iota(jnp.int32, (tok, tok), 0)
            query_at = lax.broadcasted_iota(jnp.int32, (tok, tok), 1)
            seen = seen & (key_at <= query_at)
        bias_s[...] = jnp.where(seen, 0.0, FAR)
        win_t[slot, 0] = win[slot, 0].T
        win_t[slot, 1] = win[slot, 1].T

        def scores(h):
            s = jnp.dot(win[slot, 0], qt_s[h], preferred_element_type=F32)
            s = s * (scale * log2e) + bias_s[...]
            s_s[slot, h] = s
            dp_s[slot, h] = jnp.dot(win[slot, 1], dot_s[h], preferred_element_type=F32)
            return jnp.max(eight_rows(s, jnp.maximum), axis=0, keepdims=True)

        def weigh(h, top):
            if slot:
                old = m_s[h]
                top = jnp.maximum(old, top)
                shrink = jnp.exp2(old - top)
            p = jnp.exp2(s_s[slot, h] - top)
            total = jnp.sum(eight_rows(p, jnp.add), axis=0, keepdims=True)
            out_t = jnp.dot(win_t[slot, 1], p.astype(BF16), preferred_element_type=F32)
            m_s[h] = top
            l_s[h] = l_s[h] * shrink + total if slot else total
            ot_s[h] = ot_s[h] * shrink + out_t if slot else out_t

        tops = []
        for h in range(heads + LAG):
            if h < heads:
                tops.append(scores(h))
            if h >= LAG:
                weigh(h - LAG, tops[h - LAG])

    forward(0)
    pass_on(4, (None, 8, 3, up), (y != 0, 3, 2, left), (y == 0, 7, 5, left), (y == 3, 1, 1, right), (y != 3, 5, 4, right))
    pass_on(1, (y != 3, 2, 6, right))
    forward(4)
    pass_on(8, (y != 0, 7, 5, left), (y == 3, 5, 4, right))
    pass_on(3, (y == 0, 6, 7, left))
    forward(1)
    pass_on(5, (y == 3, 2, 6, right))
    pass_on(7, (y != 0, 6, 7, left))
    forward(3)
    forward(8)
    forward(5)
    forward(7)
    pass_on(2)
    forward(2)
    pass_on(6)
    forward(6)

    for h in range(heads):
        total = l_s[h]
        out_t = (ot_s[h] * (1.0 / total)).astype(BF16)
        outt_s[h] = out_t
        d_s[h] = jnp.sum(eight_rows(dot_s[h].astype(F32) * out_t.astype(F32), jnp.add), axis=0, keepdims=True)
        m_s[h] = m_s[h] + jnp.log2(total)

    flag = phase_ref[0].astype(F32)

    def backward(slot, first_slot=False):
        dk = dv = None
        for h in range(heads):
            p = jnp.exp2(s_s[slot, h] - m_s[h])
            ds = (p * (dp_s[slot, h] - d_s[h])).astype(BF16)
            dq = jnp.dot(win_t[slot, 0], ds, preferred_element_type=F32)
            dqt_s[h] = dq if first_slot else dqt_s[h] + dq
            dk_h = jnp.dot(ds, q_s[h], preferred_element_type=F32)
            dv_h = jnp.dot(p.astype(BF16), do_s[h], preferred_element_type=F32)
            dk = dk_h if h == 0 else dk + dk_h
            dv = dv_h if h == 0 else dv + dv_h
        dk, dv = dk * (scale * flag), dv * flag
        acc[slot, 0] = acc[slot, 0] + dk if slot == 4 else dk
        acc[slot, 1] = acc[slot, 1] + dv if slot == 4 else dv

    def part(slot, half, cut, peer):
        return pltpu.make_async_remote_copy(
            src_ref=out_buf.at[slot, half, rows_of[cut]], dst_ref=in_buf.at[slot, half, rows_of[cut]],
            send_sem=bsend.at[slot, half, cut], recv_sem=brecv.at[slot, half, cut],
            device_id=peer, device_id_type=MESH)

    def send_piece(slot, half, cut, peer, when=None):
        def send():
            out_buf[slot, half, rows_of[cut]] = acc[slot, half, rows_of[cut]].astype(BF16)
            part(slot, half, cut, peer).start()

        send() if when is None else pl.when(when)(send)

    def send_part(slot, peer, when=None):
        for half, cut in pieces:
            send_piece(slot, half, cut, peer, when)

    def take_piece(slot, into, half, cut):
        part(slot, half, cut, left).wait_recv()
        rows = rows_of[cut]
        acc[into, half, rows] = acc[into, half, rows] + in_buf[slot, half, rows].astype(F32)

    acc[4] = jnp.zeros(acc.shape[1:], F32)
    backward(6, True)
    send_part(6, right)
    backward(2)
    send_part(2, left)
    backward(7)
    send_part(7, right, y == 0)
    backward(5)
    send_part(5, left, y != 3)
    backward(3)
    for half, cut in pieces:
        take_piece(6, 3 + 4 * first, half, cut)
        send_piece(7, half, cut, right, y != 0)
    send_part(3, right)
    backward(1)
    for half, cut in pieces:
        take_piece(2, 1 + 4 * last, half, cut)
        send_piece(5, half, cut, left, y == 3)
    send_part(1, left)
    backward(8)
    for half, cut in pieces:
        take_piece(7, 4 + 4 * first, half, cut)
        take_piece(5, 4 + 4 * last, half, cut)
        send_piece(8, half, cut, down)
    backward(4)
    backward(0)

    for h in range(heads):
        cols = pl.ds(h * width, width)
        o_ref[:, cols] = outt_s[h].T
        dq_ref[:, cols] = (dqt_s[h] * (scale * flag)).astype(BF16).T

    for half, cut in pieces:
        take_piece(3, 4 * first, half, cut)
        take_piece(1, 4 * last, half, cut)
        take_piece(8, 4, half, cut)
        send_piece(4, half, cut, down)
    for half, cut in pieces:
        take_piece(4, 0, half, cut)
    dk_ref[...] = acc[0, 0]
    dv_ref[...] = acc[0, 1]

    for half, cut in pieces:
        for send in range(8):
            block(0, 0, send, half, cut, left).wait_send()
        for slot in range(1, SLOTS):
            part(slot, half, cut, left).wait_send()


def solution(mesh):
    servers = mesh.shape["server"]
    tiles = servers * mesh.shape["owner"]

    def on_device(queries, key_vectors, value_vectors, out_grad, segments, phase_label):
        tok, width = key_vectors.shape
        heads = queries.shape[1] // width
        seg_rows = segments.reshape(-1, 128)
        vmem = pl.BlockSpec(memory_space=pltpu.VMEM)
        anywhere = pl.BlockSpec(memory_space=pl.ANY)
        smem = pl.BlockSpec(memory_space=pltpu.SMEM)
        return pl.pallas_call(
            functools.partial(fused, heads, 1.0 / math.sqrt(width), servers, tiles),
            out_shape=(
                jax.ShapeDtypeStruct((tok, heads * width), BF16),
                jax.ShapeDtypeStruct((tok, heads * width), BF16),
                jax.ShapeDtypeStruct((tok, width), F32),
                jax.ShapeDtypeStruct((tok, width), F32),
            ),
            in_specs=[anywhere] * 5 + [smem],
            out_specs=(vmem, vmem, vmem, vmem),
            scratch_shapes=[
                pltpu.VMEM((heads, tok, width), BF16),
                pltpu.VMEM((heads, tok, width), BF16),
                pltpu.VMEM((heads, width, tok), BF16),
                pltpu.VMEM((heads, width, tok), BF16),
                pltpu.VMEM((SLOTS, 2, tok, width), BF16),
                pltpu.VMEM((SLOTS, 2, width, tok), BF16),
                pltpu.VMEM((tiles * tok // 128, 128), jnp.int32),
                pltpu.VMEM((SLOTS, heads, tok, tok), F32),
                pltpu.VMEM((SLOTS, heads, tok, tok), F32),
                pltpu.VMEM((tok, tok), F32),
                pltpu.VMEM((heads, 1, tok), F32),
                pltpu.VMEM((heads, 1, tok), F32),
                pltpu.VMEM((heads, 1, tok), F32),
                pltpu.VMEM((heads, width, tok), F32),
                pltpu.VMEM((heads, width, tok), BF16),
                pltpu.VMEM((heads, width, tok), F32),
                pltpu.VMEM((SLOTS, 2, tok, width), F32),
                pltpu.VMEM((SLOTS, 2, tok, width), BF16),
                pltpu.VMEM((SLOTS, 2, tok, width), BF16),
                pltpu.SemaphoreType.DMA((3 + 2 * heads,)),
                pltpu.SemaphoreType.DMA((8, 2, CUTS)),
                pltpu.SemaphoreType.DMA((SLOTS, 2, CUTS)),
                pltpu.SemaphoreType.DMA((SLOTS, 2, CUTS)),
                pltpu.SemaphoreType.DMA((SLOTS, 2, CUTS)),
            ],
            compiler_params=pltpu.CompilerParams(
                collective_id=0, has_side_effects=True, vmem_limit_bytes=60 * 1024 * 1024
            ),
        )(queries, key_vectors, value_vectors, out_grad, seg_rows, phase_label)

    tokens = P(("owner", "server"), None)
    return jax.shard_map(
        on_device,
        mesh=mesh,
        in_specs=(tokens, tokens, tokens, tokens, P(), P(("owner", "server"))),
        out_specs=(tokens, tokens, tokens, tokens),
        check_vma=False,
    )
```

time: 66.2 us -> 48.4 us (0.73)
  the two profiles are of different devices: /device:TPU:97 before, /device:TPU:0 now
where the time goes in v1:
time: 48.4 us; the launch traced here: 48 us
  Pallas kernels  42.2 us (87%)
  local copies, waits for them, and re-layouts  4.56 us (9%)
  between operations  1.3 us (3%)
    pallas_call x1, Pallas kernels, on_device(): pl.pallas_call(functools.partial(fused, heads, 1.0 / math.sqrt(width), se...  42.2 us
    unnamed x10, local copies, waits for them, and re-layouts  4.56 us

profile of v1, /device:TPU:0, one launch (start us, length us, event | category | flops | bytes accessed | tf_op | source)
XLA Modules:
  0.0 48.0 jit_solution(204767263528168107)
XLA Ops:
  1.3 42.2 %shard_map.93 = (bf16[256,1024]{1,0:T(8,128)(2,1)}, bf16[256,1024]{1,0:T(8,128)(2,1)}, f32[256,128]{1,0:T(8,128)}, f32[256,128]{1,0:T(8,128)}) custom-call(bf16[256,1024]{1,0:T(8,128)(2,1)} %q_hbm.1, bf16[256,128]{1,0:T(8,128)(2,1)} %k_hbm.1, bf16[256,128]{1,0:T(8,128)(2,1)} %v_hbm.1, bf16[256,1024]{1,0:T(8,128)(2,1)} %do_hbm.1, s32[256,128]{1,0:T(8,128)} %bitcast.1, ...), custom_call_target="tpu_custom_call" | custom-call | tf_op jit(solution)/shard_map/pallas_call | solution.py:271
  43.4 0.0 copy-start
  43.4 1.9 %copy.15 = bf16[256,1024]{1,0:T(8,128)(2,1)} copy(bf16[256,1024]{1,0:T(8,128)(2,1)} %get-tuple-element.8) | data formatting | bytes 1048576
  45.4 0.0 copy-done
  45.4 0.0 copy-start.2
  45.4 0.8 %copy.16 = bf16[256,1024]{1,0:T(8,128)(2,1)} copy(bf16[256,1024]{1,0:T(8,128)(2,1)S(1)} %copy-done) | data formatting | bytes 1048576
  46.2 0.2 copy-done.2
  46.4 0.0 copy-start.1
  46.4 0.7 %copy.17 = f32[256,128]{1,0:T(8,128)} copy(f32[256,128]{1,0:T(8,128)S(1)} %copy-done.2) | data formatting | bytes 262144
  47.1 0.3 copy-done.1
  47.4 0.7 %copy.18 = f32[256,128]{1,0:T(8,128)} copy(f32[256,128]{1,0:T(8,128)S(1)} %copy-done.1) | data formatting | bytes 262144
Async XLA Ops:
  43.4 1.9 %copy-start = (bf16[256,1024]{1,0:T(8,128)(2,1)S(1)}, bf16[256,1024]{1,0:T(8,128)(2,1)}, u32[]{:S(2)}) copy-start(bf16[256,1024]{1,0:T(8,128)(2,1)} %get-tuple-element.9) | copy-start | bytes 1572868
  45.4 1.0 %copy-start.2 = (f32[256,128]{1,0:T(8,128)S(1)}, f32[256,128]{1,0:T(8,128)}, u32[]{:S(2)}) copy-start(f32[256,128]{1,0:T(8,128)} %get-tuple-element.10) | copy-start | bytes 393220
  46.4 1.0 %copy-start.1 = (f32[256,128]{1,0:T(8,128)S(1)}, f32[256,128]{1,0:T(8,128)}, u32[]{:S(2)}) copy-start(f32[256,128]{1,0:T(8,128)} %get-tuple-element.11) | copy-start | bytes 393220

commit v2 on v1

--- a/solution.py
+++ b/solution.py
@@ -66,7 +66,8 @@
             send_sem=fsend.at[send, half, cut], recv_sem=frecv.at[dst, half, cut],
             device_id=peer, device_id_type=MESH)
 
-    def pass_on(slot, *moves):
+    def pass_on(slot, *moves, between=()):
+        between = list(between)
         for half, cut in pieces:
             if slot:
                 block(slot, slot, 0, half, cut, left).wait_recv()
@@ -79,6 +80,8 @@
                     @pl.when(when)
                     def _():
                         block(slot, dst, send, half, cut, peer).start()
+            if between:
+                forward(between.pop(0))
 
     pass_on(0, (None, 4, 0, up), (y != 3, 1, 1, right), (y == 0, 3, 2, left))
 
@@ -152,10 +155,7 @@
     pass_on(3, (y == 0, 6, 7, left))
     forward(1)
     pass_on(5, (y == 3, 2, 6, right))
-    pass_on(7, (y != 0, 6, 7, left))
-    forward(3)
-    forward(8)
-    forward(5)
+    pass_on(7, (y != 0, 6, 7, left), between=(3, 8, 5))
     forward(7)
     pass_on(2)
     forward(2)
@@ -257,6 +257,16 @@
             part(slot, half, cut, left).wait_send()
 
 
+def write_out(*refs):
+    count = len(refs) // 2
+    sems = refs[-1]
+    copies = [pltpu.make_async_copy(refs[k], refs[count + k], sems.at[k]) for k in range(count)]
+    for copy in copies:
+        copy.start()
+    for copy in copies:
+        copy.wait()
+
+
 def solution(mesh):
     servers = mesh.shape["server"]
     tiles = servers * mesh.shape["owner"]
@@ -268,13 +278,13 @@
         vmem = pl.BlockSpec(memory_space=pltpu.VMEM)
         anywhere = pl.BlockSpec(memory_space=pl.ANY)
         smem = pl.BlockSpec(memory_space=pltpu.SMEM)
-        return pl.pallas_call(
+        results = pl.pallas_call(
             functools.partial(fused, heads, 1.0 / math.sqrt(width), servers, tiles),
             out_shape=(
-                jax.ShapeDtypeStruct((tok, heads * width), BF16),
-                jax.ShapeDtypeStruct((tok, heads * width), BF16),
-                jax.ShapeDtypeStruct((tok, width), F32),
-                jax.ShapeDtypeStruct((tok, width), F32),
+                pltpu.VMEM((tok, heads * width), BF16),
+                pltpu.VMEM((tok, heads * width), BF16),
+                pltpu.VMEM((tok, width), F32),
+                pltpu.VMEM((tok, width), F32),
             ),
             in_specs=[anywhere] * 5 + [smem],
             out_specs=(vmem, vmem, vmem, vmem),
@@ -305,9 +315,17 @@
                 pltpu.SemaphoreType.DMA((SLOTS, 2, CUTS)),
             ],
             compiler_params=pltpu.CompilerParams(
-                collective_id=0, has_side_effects=True, vmem_limit_bytes=60 * 1024 * 1024
+                collective_id=0, has_side_effects=True, vmem_limit_bytes=54 * 1024 * 1024
             ),
         )(queries, key_vectors, value_vectors, out_grad, seg_rows, phase_label)
+        return pl.pallas_call(
+            write_out,
+            out_shape=[jax.ShapeDtypeStruct(r.shape, r.dtype) for r in results],
+            in_specs=[vmem] * len(results),
+            out_specs=[anywhere] * len(results),
+            scratch_shapes=[pltpu.SemaphoreType.DMA((len(results),))],
+            compiler_params=pltpu.CompilerParams(vmem_limit_bytes=1024 * 1024),
+        )(*results)
 
     tokens = P(("owner", "server"), None)
     return jax.shard_map(

time: 48.4 us -> 43.9 us (0.907)
  the two profiles are of different devices: /device:TPU:0 before, /device:TPU:16 now
where the time goes in v2:
time: 43.9 us; the launch traced here: 43.8 us
  Pallas kernels  42.3 us (96%)
  between operations  1.45 us (3%)
    pallas_call x1, Pallas kernels, on_device(): pl.pallas_call(functools.partial(fused, heads, 1.0 / math.sqrt(width), se...  41.3 us
    pallas_call x1, Pallas kernels, on_device(): pl.pallas_call(write_out, out_shape=[jax.ShapeDtypeStruct(r.shape, r.dtyp...  1.08 us

profile of v2, /device:TPU:16, one launch (start us, length us, event | category | flops | bytes accessed | tf_op | source)
XLA Modules:
  0.0 43.8 jit_solution(5198544882256503925)
XLA Ops:
  1.3 41.3 %shard_map.93 = (bf16[256,1024]{1,0:T(8,128)(2,1)S(1)}, bf16[256,1024]{1,0:T(8,128)(2,1)S(1)}, f32[256,128]{1,0:T(8,128)S(1)}, f32[256,128]{1,0:T(8,128)S(1)}) custom-call(bf16[256,1024]{1,0:T(8,128)(2,1)} %q_hbm.1, bf16[256,128]{1,0:T(8,128)(2,1)} %k_hbm.1, bf16[256,128]{1,0:T(8,128)(2,1)} %v_hbm.1, bf16[256,1024]{1,0:T(8,128)(2,1)} %do_hbm.1, ...), custom_call_target="tpu_custom_call" | custom-call | tf_op jit(solution)/shard_map/pallas_call | solution.py:281
  42.5 1.1 %shard_map.94 = (bf16[256,1024]{1,0:T(8,128)(2,1)}, bf16[256,1024]{1,0:T(8,128)(2,1)}, f32[256,128]{1,0:T(8,128)}, f32[256,128]{1,0:T(8,128)}) custom-call(bf16[256,1024]{1,0:T(8,128)(2,1)S(1)} %get-tuple-element.8.refs_0_, bf16[256,1024]{1,0:T(8,128)(2,1)S(1)} %get-tuple-element.9.refs_1_, f32[256,128]{1,0:T(8,128)S(1)} %get-tuple-element.10.refs_2_, ...), custom_call_target="tpu_custom_call" | custom-call | tf_op jit(solution)/shard_map/pallas_call | solution.py:321

commit v3 on v2

--- a/solution.py
+++ b/solution.py
@@ -203,10 +203,13 @@
         for half, cut in pieces:
             send_piece(slot, half, cut, peer, when)
 
-    def take_piece(slot, into, half, cut):
-        part(slot, half, cut, left).wait_recv()
-        rows = rows_of[cut]
-        acc[into, half, rows] = acc[into, half, rows] + in_buf[slot, half, rows].astype(F32)
+    def take_piece(slot, into, half, cut, when=None):
+        def take():
+            part(slot, half, cut, left).wait_recv()
+            rows = rows_of[cut]
+            acc[into, half, rows] = acc[into, half, rows] + in_buf[slot, half, rows].astype(F32)
+
+        take() if when is None else pl.when(when)(take)
 
     acc[4] = jnp.zeros(acc.shape[1:], F32)
     backward(6, True)
@@ -230,7 +233,7 @@
     backward(8)
     for half, cut in pieces:
         take_piece(7, 4 + 4 * first, half, cut)
-        take_piece(5, 4 + 4 * last, half, cut)
+        take_piece(5, 8, half, cut, y == 3)
         send_piece(8, half, cut, down)
     backward(4)
     backward(0)
@@ -241,11 +244,13 @@
         dq_ref[:, cols] = (dqt_s[h] * (scale * flag)).astype(BF16).T
 
     for half, cut in pieces:
+        take_piece(5, 4, half, cut, y != 3)
         take_piece(3, 4 * first, half, cut)
-        take_piece(1, 4 * last, half, cut)
+        take_piece(1, 4, half, cut, y == 3)
         take_piece(8, 4, half, cut)
         send_piece(4, half, cut, down)
     for half, cut in pieces:
+        take_piece(1, 0, half, cut, y != 3)
         take_piece(4, 0, half, cut)
     dk_ref[...] = acc[0, 0]
     dv_ref[...] = acc[0, 1]
@@ -277,7 +282,6 @@
         seg_rows = segments.reshape(-1, 128)
         vmem = pl.BlockSpec(memory_space=pltpu.VMEM)
         anywhere = pl.BlockSpec(memory_space=pl.ANY)
-        smem = pl.BlockSpec(memory_space=pltpu.SMEM)
         results = pl.pallas_call(
             functools.partial(fused, heads, 1.0 / math.sqrt(width), servers, tiles),
             out_shape=(
@@ -286,7 +290,7 @@
                 pltpu.VMEM((tok, width), F32),
                 pltpu.VMEM((tok, width), F32),
             ),
-            in_specs=[anywhere] * 5 + [smem],
+            in_specs=[anywhere] * 5 + [pl.BlockSpec(memory_space=pltpu.SMEM)],
             out_specs=(vmem, vmem, vmem, vmem),
             scratch_shapes=[
                 pltpu.VMEM((heads, tok, width), BF16),

time: 43.9 us -> 43 us (0.979)
  the two profiles are of different devices: /device:TPU:16 before, /device:TPU:0 now
where the time goes in v3:
time: 43 us; the launch traced here: 42.9 us
  Pallas kernels  41.4 us (96%)
  between operations  1.45 us (3%)
    pallas_call x1, Pallas kernels, on_device(): pl.pallas_call(functools.partial(fused, heads, 1.0 / math.sqrt(width), se...  40.3 us
    pallas_call x1, Pallas kernels, on_device(): pl.pallas_call(write_out, out_shape=[jax.ShapeDtypeStruct(r.shape, r.dtyp...  1.08 us

profile of v3, /device:TPU:0, one launch (start us, length us, event | category | flops | bytes accessed | tf_op | source)
XLA Modules:
  0.0 42.9 jit_solution(6190366147258032784)
XLA Ops:
  1.3 40.3 %shard_map.93 = (bf16[256,1024]{1,0:T(8,128)(2,1)S(1)}, bf16[256,1024]{1,0:T(8,128)(2,1)S(1)}, f32[256,128]{1,0:T(8,128)S(1)}, f32[256,128]{1,0:T(8,128)S(1)}) custom-call(bf16[256,1024]{1,0:T(8,128)(2,1)} %q_hbm.1, bf16[256,128]{1,0:T(8,128)(2,1)} %k_hbm.1, bf16[256,128]{1,0:T(8,128)(2,1)} %v_hbm.1, bf16[256,1024]{1,0:T(8,128)(2,1)} %do_hbm.1, ...), custom_call_target="tpu_custom_call" | custom-call | tf_op jit(solution)/shard_map/pallas_call | solution.py:285
  41.6 1.1 %shard_map.94 = (bf16[256,1024]{1,0:T(8,128)(2,1)}, bf16[256,1024]{1,0:T(8,128)(2,1)}, f32[256,128]{1,0:T(8,128)}, f32[256,128]{1,0:T(8,128)}) custom-call(bf16[256,1024]{1,0:T(8,128)(2,1)S(1)} %get-tuple-element.8.refs_0_, bf16[256,1024]{1,0:T(8,128)(2,1)S(1)} %get-tuple-element.9.refs_1_, f32[256,128]{1,0:T(8,128)S(1)} %get-tuple-element.10.refs_2_, ...), custom_call_target="tpu_custom_call" | custom-call | tf_op jit(solution)/shard_map/pallas_call | solution.py:325

commit v4 on v3

--- a/solution.py
+++ b/solution.py
@@ -52,12 +52,14 @@
         cols = pl.ds(h * width, width)
         loads.append(pltpu.make_async_copy(q_hbm.at[:, cols], q_s.at[h], load_sem.at[3 + h]))
         loads.append(pltpu.make_async_copy(do_hbm.at[:, cols], do_s.at[h], load_sem.at[3 + heads + h]))
-    for copy in loads:
-        copy.start()
+    loads[0].start()
+    loads[1].start()
 
     barrier = pltpu.get_barrier_semaphore()
     for peer in (up, down, left, right):
         pl.semaphore_signal(barrier, inc=1, device_id=peer, device_id_type=MESH)
+    for copy in loads[2:]:
+        copy.start()
     pl.semaphore_wait(barrier, 4)
 
     def block(src, dst, send, half, cut, peer):
@@ -66,9 +68,11 @@
             send_sem=fsend.at[send, half, cut], recv_sem=frecv.at[dst, half, cut],
             device_id=peer, device_id_type=MESH)
 
-    def pass_on(slot, *moves, between=()):
+    def pass_on(slot, *moves, halves=(0, 1), between=()):
         between = list(between)
         for half, cut in pieces:
+            if half not in halves:
+                continue
             if slot:
                 block(slot, slot, 0, half, cut, left).wait_recv()
             elif cut == 0:
@@ -106,7 +110,13 @@
             total = op(total, x[k * 8:(k + 1) * 8])
         return total
 
+    tops = {}
+
     def forward(slot):
+        see_keys(slot)
+        use(slot)
+
+    def see_keys(slot):
         owner_tile = tile - slot
         k_seg = seg_row((owner_tile + tiles) % tiles)
         k_seg = jnp.where(owner_tile >= 0, k_seg, -1)
@@ -119,14 +129,21 @@
             seen = seen & (key_at <= query_at)
         bias_s[...] = jnp.where(seen, 0.0, FAR)
         win_t[slot, 0] = win[slot, 0].T
+
+    def score(slot, h):
+        s = jnp.dot(win[slot, 0], qt_s[h], preferred_element_type=F32)
+        s = s * (scale * log2e) + bias_s[...]
+        s_s[slot, h] = s
+        tops[slot, h] = jnp.max(eight_rows(s, jnp.maximum), axis=0, keepdims=True)
+
+    def use(slot):
         win_t[slot, 1] = win[slot, 1].T
+        scored = (slot, 0) in tops
 
         def scores(h):
-            s = jnp.dot(win[slot, 0], qt_s[h], preferred_element_type=F32)
-            s = s * (scale * log2e) + bias_s[...]
-            s_s[slot, h] = s
+            if not scored:
+                score(slot, h)
             dp_s[slot, h] = jnp.dot(win[slot, 1], dot_s[h], preferred_element_type=F32)
-            return jnp.max(eight_rows(s, jnp.maximum), axis=0, keepdims=True)
 
         def weigh(h, top):
             if slot:
@@ -140,12 +157,11 @@
             l_s[h] = l_s[h] * shrink + total if slot else total
             ot_s[h] = ot_s[h] * shrink + out_t if slot else out_t
 
-        tops = []
         for h in range(heads + LAG):
             if h < heads:
-                tops.append(scores(h))
+                scores(h)
             if h >= LAG:
-                weigh(h - LAG, tops[h - LAG])
+                weigh(h - LAG, tops[slot, h - LAG])
 
     forward(0)
     pass_on(4, (None, 8, 3, up), (y != 0, 3, 2, left), (y == 0, 7, 5, left), (y == 3, 1, 1, right), (y != 3, 5, 4, right))
@@ -159,8 +175,12 @@
     forward(7)
     pass_on(2)
     forward(2)
-    pass_on(6)
-    forward(6)
+    pass_on(6, halves=(0,))
+    see_keys(6)
+    for h in range(heads):
+        score(6, h)
+    pass_on(6, halves=(1,))
+    use(6)
 
     for h in range(heads):
         total = l_s[h]
@@ -171,20 +191,27 @@
 
     flag = phase_ref[0].astype(F32)
 
-    def backward(slot, first_slot=False):
+    def backward(slot, first_slot=False, keys=True, values=True):
         dk = dv = None
         for h in range(heads):
             p = jnp.exp2(s_s[slot, h] - m_s[h])
-            ds = (p * (dp_s[slot, h] - d_s[h])).astype(BF16)
-            dq = jnp.dot(win_t[slot, 0], ds, preferred_element_type=F32)
-            dqt_s[h] = dq if first_slot else dqt_s[h] + dq
-            dk_h = jnp.dot(ds, q_s[h], preferred_element_type=F32)
-            dv_h = jnp.dot(p.astype(BF16), do_s[h], preferred_element_type=F32)
-            dk = dk_h if h == 0 else dk + dk_h
-            dv = dv_h if h == 0 else dv + dv_h
-        dk, dv = dk * (scale * flag), dv * flag
-        acc[slot, 0] = acc[slot, 0] + dk if slot == 4 else dk
-        acc[slot, 1] = acc[slot, 1] + dv if slot == 4 else dv
+            if keys:
+                ds = (p * (dp_s[slot, h] - d_s[h])).astype(BF16)
+                dq = jnp.dot(win_t[slot, 0], ds, preferred_element_type=F32)
+                dqt_s[h] = dq if first_slot else dqt_s[h] + dq
+                dk_h = jnp.dot(ds, q_s[h], preferred_element_type=F32)
+                dk = dk_h if h == 0 else dk + dk_h
+            if values:
+                dv_h = jnp.dot(p.astype(BF16), do_s[h], preferred_element_type=F32)
+                dv = dv_h if h == 0 else dv + dv_h
+        if keys:
+            dk = dk * (scale * flag)
+            acc[slot, 0] = acc[slot, 0] + dk if slot == 4 else dk
+        if values:
+            dv = dv * flag
+            acc[slot, 1] = acc[slot, 1] + dv if slot == 4 else dv
+
+    back = [(half, cut) for half in (1, 0) for cut in range(CUTS)]
 
     def part(slot, half, cut, peer):
         return pltpu.make_async_remote_copy(
@@ -199,9 +226,10 @@
 
         send() if when is None else pl.when(when)(send)
 
-    def send_part(slot, peer, when=None):
-        for half, cut in pieces:
-            send_piece(slot, half, cut, peer, when)
+    def send_part(slot, peer, when=None, halves=(1, 0)):
+        for half, cut in back:
+            if half in halves:
+                send_piece(slot, half, cut, peer, when)
 
     def take_piece(slot, into, half, cut, when=None):
         def take():
@@ -212,8 +240,10 @@
         take() if when is None else pl.when(when)(take)
 
     acc[4] = jnp.zeros(acc.shape[1:], F32)
-    backward(6, True)
-    send_part(6, right)
+    backward(6, keys=False)
+    send_part(6, right, halves=(1,))
+    backward(6, True, values=False)
+    send_part(6, right, halves=(0,))
     backward(2)
     send_part(2, left)
     backward(7)
@@ -221,17 +251,17 @@
     backward(5)
     send_part(5, left, y != 3)
     backward(3)
-    for half, cut in pieces:
+    for half, cut in back:
         take_piece(6, 3 + 4 * first, half, cut)
         send_piece(7, half, cut, right, y != 0)
     send_part(3, right)
     backward(1)
-    for half, cut in pieces:
+    for half, cut in back:
         take_piece(2, 1 + 4 * last, half, cut)
         send_piece(5, half, cut, left, y == 3)
     send_part(1, left)
     backward(8)
-    for half, cut in pieces:
+    for half, cut in back:
         take_piece(7, 4 + 4 * first, half, cut)
         take_piece(5, 8, half, cut, y == 3)
         send_piece(8, half, cut, down)
@@ -243,23 +273,29 @@
         o_ref[:, cols] = outt_s[h].T
         dq_ref[:, cols] = (dqt_s[h] * (scale * flag)).astype(BF16).T
 
-    for half, cut in pieces:
+    for half, cut in back:
+        for send in range(8):
+            block(0, 0, send, half, cut, left).wait_send()
+        for slot in (2, 5, 6, 7):
+            part(slot, half, cut, left).wait_send()
+
+    for half, cut in back:
         take_piece(5, 4, half, cut, y != 3)
         take_piece(3, 4 * first, half, cut)
         take_piece(1, 4, half, cut, y == 3)
         take_piece(8, 4, half, cut)
         send_piece(4, half, cut, down)
-    for half, cut in pieces:
+    for half, cut in back:
         take_piece(1, 0, half, cut, y != 3)
-        take_piece(4, 0, half, cut)
-    dk_ref[...] = acc[0, 0]
-    dv_ref[...] = acc[0, 1]
-
-    for half, cut in pieces:
-        for send in range(8):
-            block(0, 0, send, half, cut, left).wait_send()
-        for slot in range(1, SLOTS):
+        for slot in (1, 3, 8):
             part(slot, half, cut, left).wait_send()
+    for half, cut in back:
+        part(4, half, cut, left).wait_recv()
+        rows = rows_of[cut]
+        grad_ref = (dk_ref, dv_ref)[half]
+        grad_ref[rows, :] = acc[0, half, rows] + in_buf[4, half, rows].astype(F32)
+    for half, cut in back:
+        part(4, half, cut, left).wait_send()
 
 
 def write_out(*refs):

time: 43 us -> 43.4 us (level)
  no operation moved by 1% of the time
where the time goes in v4:
time: 43.4 us; the launch traced here: 43.3 us
  Pallas kernels  41.8 us (96%)
  between operations  1.45 us (3%)
    pallas_call x1, Pallas kernels, on_device(): pl.pallas_call(functools.partial(fused, heads, 1.0 / math.sqrt(width), se...  40.7 us
    pallas_call x1, Pallas kernels, on_device(): pl.pallas_call(write_out, out_shape=[jax.ShapeDtypeStruct(r.shape, r.dtyp...  1.08 us

profile of v4, /device:TPU:0, one launch (start us, length us, event | category | flops | bytes accessed | tf_op | source)
XLA Modules:
  0.0 43.3 jit_solution(722477465813291649)
XLA Ops:
  1.3 40.7 %shard_map.93 = (bf16[256,1024]{1,0:T(8,128)(2,1)S(1)}, bf16[256,1024]{1,0:T(8,128)(2,1)S(1)}, f32[256,128]{1,0:T(8,128)S(1)}, f32[256,128]{1,0:T(8,128)S(1)}) custom-call(bf16[256,1024]{1,0:T(8,128)(2,1)} %q_hbm.1, bf16[256,128]{1,0:T(8,128)(2,1)} %k_hbm.1, bf16[256,128]{1,0:T(8,128)(2,1)} %v_hbm.1, bf16[256,1024]{1,0:T(8,128)(2,1)} %do_hbm.1, ...), custom_call_target="tpu_custom_call" | custom-call | tf_op jit(solution)/shard_map/pallas_call | solution.py:321
  42.0 1.1 %shard_map.94 = (bf16[256,1024]{1,0:T(8,128)(2,1)}, bf16[256,1024]{1,0:T(8,128)(2,1)}, f32[256,128]{1,0:T(8,128)}, f32[256,128]{1,0:T(8,128)}) custom-call(bf16[256,1024]{1,0:T(8,128)(2,1)S(1)} %get-tuple-element.8.refs_0_, bf16[256,1024]{1,0:T(8,128)(2,1)S(1)} %get-tuple-element.9.refs_1_, f32[256,128]{1,0:T(8,128)S(1)} %get-tuple-element.10.refs_2_, ...), custom_call_target="tpu_custom_call" | custom-call | tf_op jit(solution)/shard_map/pallas_call | solution.py:361

commit v5 on v3

--- a/solution.py
+++ b/solution.py
@@ -52,12 +52,14 @@
         cols = pl.ds(h * width, width)
         loads.append(pltpu.make_async_copy(q_hbm.at[:, cols], q_s.at[h], load_sem.at[3 + h]))
         loads.append(pltpu.make_async_copy(do_hbm.at[:, cols], do_s.at[h], load_sem.at[3 + heads + h]))
-    for copy in loads:
-        copy.start()
+    loads[0].start()
+    loads[1].start()
 
     barrier = pltpu.get_barrier_semaphore()
     for peer in (up, down, left, right):
         pl.semaphore_signal(barrier, inc=1, device_id=peer, device_id_type=MESH)
+    for copy in loads[2:]:
+        copy.start()
     pl.semaphore_wait(barrier, 4)
 
     def block(src, dst, send, half, cut, peer):
@@ -244,6 +246,12 @@
         dq_ref[:, cols] = (dqt_s[h] * (scale * flag)).astype(BF16).T
 
     for half, cut in pieces:
+        for send in range(8):
+            block(0, 0, send, half, cut, left).wait_send()
+        for slot in (2, 5, 6, 7):
+            part(slot, half, cut, left).wait_send()
+
+    for half, cut in pieces:
         take_piece(5, 4, half, cut, y != 3)
         take_piece(3, 4 * first, half, cut)
         take_piece(1, 4, half, cut, y == 3)
@@ -251,15 +259,15 @@
         send_piece(4, half, cut, down)
     for half, cut in pieces:
         take_piece(1, 0, half, cut, y != 3)
-        take_piece(4, 0, half, cut)
-    dk_ref[...] = acc[0, 0]
-    dv_ref[...] = acc[0, 1]
-
-    for half, cut in pieces:
-        for send in range(8):
-            block(0, 0, send, half, cut, left).wait_send()
-        for slot in range(1, SLOTS):
+        for slot in (1, 3, 8):
             part(slot, half, cut, left).wait_send()
+    for half, cut in pieces:
+        part(4, half, cut, left).wait_recv()
+        rows = rows_of[cut]
+        grad_ref = (dk_ref, dv_ref)[half]
+        grad_ref[rows, :] = acc[0, half, rows] + in_buf[4, half, rows].astype(F32)
+    for half, cut in pieces:
+        part(4, half, cut, left).wait_send()
 
 
 def write_out(*refs):

time: 43 us -> 43 us (level)
  no operation moved by 1% of the time
where the time goes in v5:
time: 43 us; the launch traced here: 42.9 us
  Pallas kernels  41.4 us (96%)
  between operations  1.45 us (3%)
    pallas_call x1, Pallas kernels, on_device(): pl.pallas_call(functools.partial(fused, heads, 1.0 / math.sqrt(width), se...  40.4 us
    pallas_call x1, Pallas kernels, on_device(): pl.pallas_call(write_out, out_shape=[jax.ShapeDtypeStruct(r.shape, r.dtyp...  1.08 us

profile of v5, /device:TPU:0, one launch (start us, length us, event | category | flops | bytes accessed | tf_op | source)
XLA Modules:
  0.0 42.9 jit_solution(4118245508233994111)
XLA Ops:
  1.3 40.4 %shard_map.93 = (bf16[256,1024]{1,0:T(8,128)(2,1)S(1)}, bf16[256,1024]{1,0:T(8,128)(2,1)S(1)}, f32[256,128]{1,0:T(8,128)S(1)}, f32[256,128]{1,0:T(8,128)S(1)}) custom-call(bf16[256,1024]{1,0:T(8,128)(2,1)} %q_hbm.1, bf16[256,128]{1,0:T(8,128)(2,1)} %k_hbm.1, bf16[256,128]{1,0:T(8,128)(2,1)} %v_hbm.1, bf16[256,1024]{1,0:T(8,128)(2,1)} %do_hbm.1, ...), custom_call_target="tpu_custom_call" | custom-call | tf_op jit(solution)/shard_map/pallas_call | solution.py:293
  41.7 1.1 %shard_map.94 = (bf16[256,1024]{1,0:T(8,128)(2,1)}, bf16[256,1024]{1,0:T(8,128)(2,1)}, f32[256,128]{1,0:T(8,128)}, f32[256,128]{1,0:T(8,128)}) custom-call(bf16[256,1024]{1,0:T(8,128)(2,1)S(1)} %get-tuple-element.8.refs_0_, bf16[256,1024]{1,0:T(8,128)(2,1)S(1)} %get-tuple-element.9.refs_1_, f32[256,128]{1,0:T(8,128)S(1)} %get-tuple-element.10.refs_2_, ...), custom_call_target="tpu_custom_call" | custom-call | tf_op jit(solution)/shard_map/pallas_call | solution.py:333
